TPU v7x, 256 devices: a whole 4x4x8 slice. The times are simulated.
256 devices in a mesh: clip: 32 (over z_lo, y, core), row: 2 (over z_hi), src: 4 (over x).
Axes of the slice: x: 4, y: 4, z: 8 (z_hi: 2, z_lo: 4; z = z_hi * 4 + z_lo), core: 2. Of those that a mesh axis runs over, the one named last changes fastest.
Arguments:
- mask_clip: bfloat16 [131072, 4096], P(('clip', 'row'), 'src'), parts along dimension 0, may hold values from -6 to 6
- source_shifts: int32 [16, 2], P('src'), may hold values from -64 to 64
- source_weights: int32 [16], P('src'), may hold values from 1 to 8
Outputs:
- intensity: float32 [32768, 1024], P(('clip', 'row', 'src')), parts along dimension 0
There are 32 independent parts, one for each index of `clip`. A program takes and returns all parts, laid end to end along the dimension named above; an argument that names none is the same for every part. Nothing has to cross between parts.
All inputs are finite; a program needn't handle non-finite values.
Results may differ from a plain program's by a relative error of at most 0.0052.
Values may be sent and summed in bfloat16 or wider, within the bound.
No kernel may reach another device: no remote copies, remote signals or barrier semaphores. Data moves between devices by JAX's collectives and lax.ppermute only.
A program may use at most 64 MiB of HBM per device.

v0:
```python
import math
import jax
import jax.numpy as jnp
from jax import lax
from jax.sharding import PartitionSpec as P

NM = 4096
P_SIZE = 256
NI = 1024


def twiddles(positions, length, scaling):
    frequency = jnp.arange(P_SIZE, dtype=jnp.int32) - P_SIZE // 2
    product = jnp.mod(positions[:, None] * frequency[None, :], length)
    angles = product.astype(jnp.float32) * jnp.float32(2.0 * math.pi / length)
    return (jnp.cos(angles) * jnp.float32(scaling), jnp.sin(angles) * jnp.float32(scaling))


def tile_spectrum(mask_tile, row_first, col_first):
    row_index = row_first + jnp.arange(mask_tile.shape[0], dtype=jnp.int32)
    col_index = col_first + jnp.arange(mask_tile.shape[1], dtype=jnp.int32)
    col_cos, col_sin = twiddles(col_index, NM, 1.0 / math.sqrt(NM))
    col_table = jnp.concatenate([col_cos, -col_sin], 1).astype(jnp.bfloat16)
    half_way = jnp.dot(mask_tile, col_table, preferred_element_type=jnp.float32).astype(
        jnp.bfloat16
    )
    row_cos, row_sin = twiddles(row_index, NM, 1.0 / math.sqrt(NM))
    row_table = jnp.concatenate([row_cos, row_sin], 1).T.astype(jnp.bfloat16)
    blocks = jnp.dot(row_table, half_way, preferred_element_type=jnp.float32)
    real_part = blocks[:P_SIZE, :P_SIZE] + blocks[P_SIZE:, P_SIZE:]
    imag_part = blocks[:P_SIZE, P_SIZE:] - blocks[P_SIZE:, :P_SIZE]
    return jnp.stack([real_part, imag_part])


def build_left(image_rows):
    row_cos, row_sin = twiddles(image_rows, NI, 1.0 / math.sqrt(P_SIZE))
    return jnp.concatenate([row_cos, row_sin], 0).astype(jnp.bfloat16)


def build_right():
    col_cos, col_sin = twiddles(jnp.arange(NI, dtype=jnp.int32), NI, 1.0 / math.sqrt(P_SIZE))
    upper = jnp.concatenate([col_cos.T, col_sin.T], 1)
    lower = jnp.concatenate([-col_sin.T, col_cos.T], 1)
    return jnp.concatenate([upper, lower], 0).astype(jnp.bfloat16)


def source_image(spectrum, shift_pair, weight, left_table, right_table):
    frequency = jnp.arange(P_SIZE, dtype=jnp.int32) - P_SIZE // 2
    along_rows = frequency + shift_pair[0]
    along_cols = frequency + shift_pair[1]
    radius = P_SIZE // 4
    inside = (
        along_rows[:, None] * along_rows[:, None] + along_cols[None, :] * along_cols[None, :]
        <= radius * radius
    )
    pupil_mask = inside.astype(jnp.bfloat16)
    passed = jnp.concatenate([spectrum[0] * pupil_mask, spectrum[1] * pupil_mask], 1)
    blocks = jnp.dot(left_table, passed, preferred_element_type=jnp.float32)
    row_count = left_table.shape[0] // 2
    k_real = blocks[:row_count, :P_SIZE] - blocks[row_count:, P_SIZE:]
    k_imag = blocks[:row_count, P_SIZE:] + blocks[row_count:, :P_SIZE]
    partial_value = jnp.concatenate([k_real, k_imag], 1).astype(jnp.bfloat16)
    field_pair = jnp.dot(partial_value, right_table, preferred_element_type=jnp.float32)
    field_real = field_pair[:, :NI]
    field_imag = field_pair[:, NI:]
    return weight.astype(jnp.float32) * (field_real * field_real + field_imag * field_imag)


def image_rows_sum(spectrum, image_rows, all_shifts, all_weights, right_table):
    left_table = build_left(image_rows)

    def add_source(running, source_item):
        shift_pair, weight = source_item
        return (running + source_image(spectrum, shift_pair, weight, left_table, right_table), None)

    summed, _ = lax.scan(
        add_source, jnp.zeros((image_rows.shape[0], NI), jnp.float32), (all_shifts, all_weights)
    )
    return summed


def body(mask_clip, source_shifts, source_weights):
    row_id = lax.axis_index("row")
    src_id = lax.axis_index("src")
    strip_rows = mask_clip.shape[0]
    strip_cols = mask_clip.shape[1]
    partial_value = tile_spectrum(mask_clip, row_id * strip_rows, src_id * strip_cols)
    spectrum = lax.psum(partial_value, ("row", "src")).astype(jnp.bfloat16)
    right_table = build_right()
    image_strip = NI // lax.axis_size("row")
    rows_dev = image_strip // lax.axis_size("src")
    sources = source_shifts.shape[0] * lax.axis_size("src")
    image_rows = row_id * image_strip + jnp.arange(rows_dev * lax.axis_size("src"), dtype=jnp.int32)
    summed = lax.psum_scatter(
        image_rows_sum(spectrum, image_rows, source_shifts, source_weights, right_table),
        "src",
        scatter_dimension=0,
        tiled=True,
    )
    return summed / jnp.float32(sources)


def solution(mesh):
    placed = (P(("clip", "row"), "src"), P("src", None), P("src"))
    return jax.shard_map(
        body, mesh=mesh, in_specs=placed, out_specs=P(("clip", "row", "src"), None), check_vma=False
    )
```

profile of v0, /device:TPU:1, one launch (start us, length us, event | category | flops | bytes accessed | tf_op | source)
XLA Modules:
  0.0 177.1 jit_solution(12008709048086519349)
XLA Ops:
  6.6 5.7 %fusion.35 = (bf16[256,1024]{1,0:T(8,128)(2,1)S(1)}, bf16[256,1024]{1,0:T(8,128)(2,1)}, bf16[256,1024]{1,0:T(8,128)(2,1)}) fusion(s32[256]{0:T(256)S(1)} %iota_add_fusion.4), kind=kLoop, calls=%fused_computation.70 | loop fusion | flops 5242880 | bytes 1573888 | tf_op jit(solution)/shard_map/convert.7
  12.3 3.2 %multiply_convert_fusion.5 = (bf16[512,256]{1,0:T(8,128)(2,1)}, bf16[512,256]{1,0:T(8,128)(2,1)}) fusion(s32[256]{0:T(256)S(1)} %iota_add_fusion.4, s32[512]{0:T(512)S(1)} %iota_add_fusion.3), kind=kLoop, calls=%fused_computation.79 | loop fusion | flops 2359296 | bytes 527360 | tf_op jit(solution)/shard_map/convert.8
  15.5 5.6 %multiply_convert_fusion.3 = (bf16[1024,256]{1,0:T(8,128)(2,1)S(1)}, bf16[1024,256]{1,0:T(8,128)(2,1)}) fusion(s32[256]{0:T(256)S(1)} %iota_add_fusion.4, s32[1024]{0:T(1024)S(1)} %iota_add_fusion.2), kind=kLoop, calls=%fused_computation.65 | loop fusion | flops 4980736 | bytes 1053696 | tf_op jit(solution)/shard_map/convert.10
  21.1 10.2 %multiply_convert_fusion.1 = (bf16[2048,256]{1,0:T(8,128)(2,1)}, bf16[2048,256]{1,0:T(8,128)(2,1)}) fusion(s32[256]{0:T(256)S(1)} %iota_add_fusion.4, s32[2048]{0:T(1024)S(1)} %iota_add_fusion.1), kind=kLoop, calls=%fused_computation.41 | loop fusion | flops 9437184 | bytes 2106368 | tf_op jit(solution)/shard_map/convert.12
  31.3 7.5 %fusion.19 = f32[512,512]{1,0:T(8,128)} fusion(bf16[2048,256]{1,0:T(8,128)(2,1)} %get-tuple-element.144, bf16[2048,256]{1,0:T(8,128)(2,1)} %get-tuple-element.143, bf16[2048,1024]{1,0:T(8,128)(2,1)} %param.5, bf16[1024,256]{1,0:T(8,128)(2,1)} %get-tuple-element.146, bf16[1024,256]{1,0:T(8,128)(2,1)S(1)} %get-tuple-element.145), kind=kOutput, calls=%fused_computation.35 | convolution fusion | flops 3228565504 | bytes 8388608 | tf_op jit(solution)/shard_map/dot_general | solution.py:29
  38.8 1.3 fusion.42
  40.1 63.6 %all-reduce.1 = bf16[2,256,256]{2,1,0:T(8,128)(2,1)S(1)} all-reduce(f32[2,256,256]{2,1,0:T(8,128)S(1)} %pad_maximum_fusion), channel_id=1, replica_groups=mesh['clip'=32,'row'=2,'src'=4] {'row','src'}, use_global_device_ids=true, to_apply=%region_0.1 | all-reduce | flops 131072 | bytes 786432 | tf_op jit(solution)/shard_map/psum | solution.py:88
  104.8 2.9 %maximum_maximum_fusion = bf16[512,2048]{1,0:T(8,128)(2,1)} fusion(bf16[256,1024]{1,0:T(8,128)(2,1)} %get-tuple-element.151, bf16[256,1024]{1,0:T(8,128)(2,1)} %get-tuple-element.150, bf16[256,1024]{1,0:T(8,128)(2,1)S(1)} %get-tuple-element.149), kind=kLoop, calls=%fused_computation.39 | loop fusion | flops 8388608 | bytes 3670016 | tf_op jit(solution)/shard_map/concatenate | solution.py:44
  107.7 29.0 %while.13 = (s32[]{:T(128)}, f32[512,1024]{1,0:T(8,128)S(1)}, s32[4]{0:T(128)S(1)}, s32[4,2]{0,1:T(2,128)S(1)}, bf16[2,256,256]{2,1,0:T(8,128)(2,1)S(1)}, /*inde...) while((s32[]{:T(128)}, f32[512,1024]{1,0:T(8,128)S(1)}, ...), condition=%wide.region_2.3_spmd.clone, body=%wide.region_1.2_spmd.clone.sunk | while | flops 1347683584 | bytes 29626572 | solution.py:76
  109.5 1.2 add_multiply_fusion.3
  112.5 1.3 fusion.65
  113.8 1.2 fusion.66
  116.8 1.2 add_multiply_fusion.3
  119.7 1.3 fusion.65
  121.0 1.2 fusion.66
  124.1 1.2 add_multiply_fusion.3
  127.0 1.3 fusion.65
  128.3 1.2 fusion.66
  131.3 1.2 add_multiply_fusion.3
  134.3 1.3 fusion.65
  135.6 1.2 fusion.66
  136.8 1.3 copy-done
  138.1 30.2 %reduce-scatter.2.cloned.1.call-done = f32[128,1024]{1,0:T(8,128)} async-done(((f32[512,1024]{1,0:T(8,128)}), f32[128,1024]{1,0:T(8,128)}) %reduce-scatter.2.cloned.1.call-update) | async-done | bytes 524304 | tf_op jit(solution)/shard_map/reduce_scatter | solution.py:94
  168.3 1.9 %broadcast_multiply_fusion = f32[128,1024]{1,0:T(8,128)} fusion(f32[128,1024]{1,0:T(8,128)} %reduce-scatter.2.cloned.1.call-done), kind=kLoop, calls=%fused_computation.84 | loop fusion | flops 131072 | bytes 1048576 | tf_op jit(solution)/shard_map/div | solution.py:100
  (46 shorter events, 12.6 us)
Async XLA Ops:
  6.5 161.8 %reduce-scatter.2.cloned.1.call-start = ((), (), s32[]{:S(2)}) async-start(), calls=%async_computation.1 | async-start | bytes 2621440 | tf_op jit(solution)/shard_map/reduce_scatter | solution.py:94
  104.8 2.9 %copy-start.2 = (s32[4,2]{0,1:T(2,128)S(1)}, s32[4,2]{0,1:T(2,128)}, u32[]{:S(2)}) copy-start(s32[4,2]{0,1:T(2,128)} %param.6) | copy-start | bytes 100
  104.8 2.9 %copy-start.3 = (s32[4]{0:T(128)S(1)}, s32[4]{0:T(128)}, u32[]{:S(2)}) copy-start(s32[4]{0:T(128)} %param.7) | copy-start | bytes 52
  110.9 1.6 copy-start.1
  118.1 1.6 copy-start.1
  125.4 1.6 copy-start.1
  132.7 1.6 copy-start.1
  136.8 1.3 copy-start
Sparse Core Ops, SparseCore 0:
  138.2 30.0 reduce-scatter.1
where the time goes:
time: 178 us; the launch traced here: 177 us
  blocking collectives  63.6 us (36%)
  other arithmetic  42.6 us (24%)
  waiting for transfers between devices  30.2 us (17%)
  matrix products  14.5 us (8%)
  between operations  13.5 us (8%)
  local copies, waits for them, and re-layouts  9.76 us (5%)
  loops' own time  2.82 us (2%)
    psum x1, blocking collectives, body(): spectrum = lax.psum(partial_value, ('row', 'src')).astype(jnp.bfloat16)  63.6 us
    reduce_scatter x1, waiting for transfers between devices, body(): lax.psum_scatter(image_rows_sum(spectrum, image_rows, source_shifts, sour...  30.2 us
    another operation x8, other arithmetic  25.4 us
    dot_general x1, matrix products, tile_spectrum(): blocks = jnp.dot(row_table, half_way, preferred_element_type=jnp.float32)  7.46 us
    dot_general x4, matrix products, source_image(): jnp.dot(partial_value, right_table, preferred_element_type=jnp.float32)  5.14 us
    add x4, other arithmetic, add_source(): running + source_image(spectrum, shift_pair, weight, left_table, right_ta...  4.83 us
    mul x4, other arithmetic, source_image(): along_cols[None, :] * along_cols[None, :]  4.79 us
    while x8, local copies, waits for them, and re-layouts  3.71 us
  transfers between devices with their start and end apart: 1, of which 1 were waited for; matrix products, arithmetic and copies ran while one was open for 0% of the time, Pallas kernels for 0%

commit v1 on v0

--- a/solution.py
+++ b/solution.py
@@ -85,7 +85,7 @@
     strip_rows = mask_clip.shape[0]
     strip_cols = mask_clip.shape[1]
     partial_value = tile_spectrum(mask_clip, row_id * strip_rows, src_id * strip_cols)
-    spectrum = lax.psum(partial_value, ("row", "src")).astype(jnp.bfloat16)
+    spectrum = jnp.sum(lax.all_gather(partial_value, ("row", "src")), axis=0).astype(jnp.bfloat16)
     right_table = build_right()
     image_strip = NI // lax.axis_size("row")
     rows_dev = image_strip // lax.axis_size("src")

time: 178 us -> 209 us (1.17)
  waiting for transfers between devices: 30.2 us -> 129 us
  blocking collectives: 63.6 us -> 0 us
  other arithmetic: 42.6 us -> 40.5 us
    all_gather x0 -> x1, waiting for transfers between devices: none -> 101 us  [body(): lax.all_gather(partial_value, ('row', 'src'))]
    psum x1 -> x0, blocking collectives: 63.6 us -> none  [body(): spectrum = lax.psum(partial_value, ('row', 'src')).astype(jnp.bfloat16)]
    reduce_scatter x1, waiting for transfers between devices: 30.2 us -> 27.7 us  [body(): lax.psum_scatter(image_rows_sum(spectrum, image_rows, source_shifts, sour...]
    reduce_sum x0 -> x1, other arithmetic: none -> 2.51 us  [body(): jnp.sum(lax.all_gather(partial_value, ('row', 'src')), axis=0)]
  transfers between devices with their start and end apart: 1 -> 2, of which waited for: 1 -> 2; matrix products, arithmetic and copies ran while one was open for 0% -> 4% of each run, Pallas kernels for 0% -> 0%
where the time goes in v1:
time: 209 us
  waiting for transfers between devices  129 us (62%)
  other arithmetic  40.5 us (19%)
  between operations  13.5 us (6%)
  matrix products  13.1 us (6%)
  local copies, waits for them, and re-layouts  10 us (5%)
  loops' own time  2.83 us (1%)
    all_gather x1, waiting for transfers between devices, body(): lax.all_gather(partial_value, ('row', 'src'))  101 us
    reduce_scatter x1, waiting for transfers between devices, body(): lax.psum_scatter(image_rows_sum(spectrum, image_rows, source_shifts, sour...  27.7 us
    another operation x8, other arithmetic  23.3 us
    dot_general x1, matrix products, tile_spectrum(): blocks = jnp.dot(row_table, half_way, preferred_element_type=jnp.float32)  5.99 us
    dot_general x4, matrix products, source_image(): jnp.dot(partial_value, right_table, preferred_element_type=jnp.float32)  5.14 us
    mul x4, other arithmetic, source_image(): along_cols[None, :] * along_cols[None, :]  5.08 us
    add x4, other arithmetic, add_source(): running + source_image(spectrum, shift_pair, weight, left_table, right_ta...  4.83 us
  transfers between devices with their start and end apart: 2, of which 2 were waited for; matrix products, arithmetic and copies ran while one was open for 4% of the time, Pallas kernels for 0%

profile of v1, /device:TPU:1, one launch (start us, length us, event | category | flops | bytes accessed | tf_op | source)
XLA Modules:
  0.0 208.9 jit_solution(8015263370144460074)
XLA Ops:
  6.5 5.7 %multiply_convert_fusion.3 = (bf16[1024,256]{1,0:T(8,128)(2,1)}, bf16[1024,256]{1,0:T(8,128)(2,1)}) fusion(s32[256]{0:T(256)S(1)} %iota_add_fusion.4, s32[1024]{0:T(1024)S(1)} %iota_add_fusion.2), kind=kLoop, calls=%fused_computation.65 | loop fusion | flops 4980736 | bytes 1053696 | tf_op jit(solution)/shard_map/convert.10
  12.3 9.5 %multiply_convert_fusion.1 = (bf16[2048,256]{1,0:T(8,128)(2,1)S(1)}, bf16[2048,256]{1,0:T(8,128)(2,1)S(1)}) fusion(s32[256]{0:T(256)S(1)} %iota_add_fusion.4, s32[2048]{0:T(1024)S(1)} %iota_add_fusion.1), kind=kLoop, calls=%fused_computation.41 | loop fusion | flops 9437184 | bytes 2106368 | tf_op jit(solution)/shard_map/convert.12
  21.8 6.0 %fusion.19 = f32[512,512]{1,0:T(8,128)S(1)} fusion(bf16[2048,256]{1,0:T(8,128)(2,1)S(1)} %get-tuple-element.144, bf16[2048,256]{1,0:T(8,128)(2,1)S(1)} %get-tuple-element.143, bf16[2048,1024]{1,0:T(8,128)(2,1)} %param.5, bf16[1024,256]{1,0:T(8,128)(2,1)} %get-tuple-element.146, bf16[1024,256]{1,0:T(8,128)(2,1)} %get-tuple-element.145), kind=kOutput, calls=%fused_computation.35 | convolution fusion | flops 3228565504 | bytes 8388608 | tf_op jit(solution)/shard_map/dot_general | solution.py:29
  28.8 2.5 %multiply_convert_fusion.5 = (bf16[512,256]{1,0:T(8,128)(2,1)S(1)}, bf16[512,256]{1,0:T(8,128)(2,1)S(1)}) fusion(s32[256]{0:T(256)S(1)} %iota_add_fusion.4, s32[512]{0:T(512)S(1)} %iota_add_fusion.3), kind=kLoop, calls=%fused_computation.79 | loop fusion | flops 2359296 | bytes 527360 | tf_op jit(solution)/shard_map/convert.8
  31.3 4.9 %fusion.35 = (bf16[256,1024]{1,0:T(8,128)(2,1)S(1)}, bf16[256,1024]{1,0:T(8,128)(2,1)S(1)}, bf16[256,1024]{1,0:T(8,128)(2,1)S(1)}) fusion(s32[256]{0:T(256)S(1)} %iota_add_fusion.4), kind=kLoop, calls=%fused_computation.70 | loop fusion | flops 5242880 | bytes 1573888 | tf_op jit(solution)/shard_map/convert.7
  36.3 1.5 maximum_maximum_fusion
  37.8 101.2 %all-gather.3.cloned.1.call-done = f32[16,256,256]{2,1,0:T(8,128)} async-done(((f32[2,256,256]{2,1,0:T(8,128)}), f32[16,256,256]{2,1,0:T(8,128)}) %all-gather.3.cloned.1.call-update) | async-done | bytes 4194320 | tf_op jit(solution)/shard_map/all_gather | solution.py:88
  139.0 2.5 %reduce_sum.9 = bf16[2,256,256]{2,1,0:T(8,128)(2,1)S(1)} reduce(f32[8,2,256,256]{3,2,1,0:T(8,128)} %bitcast.31, f32[]{:T(128)} %constant.94.clone.1), dimensions={0}, to_apply=%region_0.1 | reduce | flops 917504 | bytes 4456452 | tf_op jit(solution)/shard_map/reduce_sum | solution.py:88
  141.5 29.6 %while.13 = (s32[]{:T(128)}, f32[512,1024]{1,0:T(8,128)S(1)}, s32[4]{0:T(128)S(1)}, s32[4,2]{0,1:T(2,128)S(1)}, bf16[2,256,256]{2,1,0:T(8,128)(2,1)S(1)}, /*inde...) while((s32[]{:T(128)}, f32[512,1024]{1,0:T(8,128)S(1)}, ...), condition=%wide.region_2.3_spmd.clone, body=%wide.region_1.2_spmd.clone.sunk | while | flops 1347683584 | bytes 29626572 | solution.py:76
  143.4 1.3 add_multiply_fusion.3
  146.4 1.3 fusion.65
  147.7 1.2 fusion.66
  150.8 1.3 add_multiply_fusion.3
  153.8 1.3 fusion.65
  155.1 1.2 fusion.66
  158.2 1.3 add_multiply_fusion.3
  161.2 1.3 fusion.65
  162.5 1.2 fusion.66
  165.6 1.3 add_multiply_fusion.3
  168.6 1.3 fusion.65
  169.9 1.2 fusion.66
  171.1 1.3 copy-done
  172.5 27.7 %reduce-scatter.2.cloned.1.call-done = f32[128,1024]{1,0:T(8,128)} async-done(((f32[512,1024]{1,0:T(8,128)}), f32[128,1024]{1,0:T(8,128)}) %reduce-scatter.2.cloned.1.call-update) | async-done | bytes 524304 | tf_op jit(solution)/shard_map/reduce_scatter | solution.py:94
  200.2 1.9 broadcast_multiply_fusion
  (49 shorter events, 12.8 us)
Async XLA Ops:
  6.5 132.4 %all-gather.3.cloned.1.call-start = ((), (), s32[]{:S(2)}) async-start(), calls=%async_computation.2 | async-start | bytes 4718592 | tf_op jit(solution)/shard_map/all_gather | solution.py:88
  28.7 171.5 %reduce-scatter.2.cloned.1.call-start = ((), (), s32[]{:S(2)}) async-start(), calls=%async_computation.1 | async-start | bytes 2621440 | tf_op jit(solution)/shard_map/reduce_scatter | solution.py:94
  139.0 2.5 %copy-start.2 = (s32[4,2]{0,1:T(2,128)S(1)}, s32[4,2]{0,1:T(2,128)}, u32[]{:S(2)}) copy-start(s32[4,2]{0,1:T(2,128)} %param.6) | copy-start | bytes 100
  139.0 2.5 %copy-start.3 = (s32[4]{0:T(128)S(1)}, s32[4]{0:T(128)}, u32[]{:S(2)}) copy-start(s32[4]{0:T(128)} %param.7) | copy-start | bytes 52
  144.8 1.6 copy-start.1
  152.2 1.6 copy-start.1
  159.6 1.6 copy-start.1
  167.0 1.6 copy-start.1
  171.1 1.3 copy-start
Sparse Core Ops, SparseCore 0:
  28.8 110.1 all-gather.2
  172.6 27.5 reduce-scatter.1
